TPU v7x, 128 devices: a whole 4x4x4 slice. The times are simulated.
128 devices in a mesh: ctx: 16 (over z_lo, x, core), tp: 8 (over y, z_hi).
Axes of the slice: x: 4, y: 4, z: 4 (z_hi: 2, z_lo: 2; z = z_hi * 2 + z_lo), core: 2. Of those that a mesh axis runs over, the one named last changes fastest.
Arguments:
- queries: bfloat16 [2048, 16384], P('ctx', 'tp'), may hold values from -110 to 110
- key_value_cache: bfloat16 [2, 10240, 1024], P(None, 'ctx', 'tp'), may hold values from -9 to 9
- cache_lengths: int32 [16], P('ctx'), may hold values from 64 to 512, as said below
- token_order: int32 [2048], P('ctx'), may hold values from 0 to 2047, each once
- out_weight: bfloat16 [16384, 16384], P('tp', 'ctx'), may hold values from -0.046875 to 0.046875
Outputs:
- output: bfloat16 [2048, 16384], P('tp', 'ctx')
Inputs may be any that keep to these rules, and one draw needn't show every extreme that they name: `cache_lengths`: one shard's cache is full in every draw. `token_order`: each number of 0 to 2047 stands once.
All inputs are finite; a program needn't handle non-finite values.
Results may differ from a plain program's by a relative error of at most 0.04.
Values may be sent and summed in bfloat16 or wider, within the bound.
No kernel may reach another device: no remote copies, remote signals or barrier semaphores. Data moves between devices by JAX's collectives and lax.ppermute only.
A program may use at most 64 MiB of HBM per device.

v0:
```python
import math

import jax
import jax.numpy as jnp
from jax import lax
from jax.sharding import Mesh
from jax.sharding import PartitionSpec as P

QUERY_HEADS = 128
KEY_VALUE_HEADS = 8
HEAD_SIZE = 128
TOKENS_PER_SHARD = 128
CACHE_DEV = 512
SHARD_ROWS = 640
TP = ("tp_0", "tp_1")


masked_floor = -1e30
key_block = 512


def scatter_axes(shard, axes, dim):
    if not axes:
        return shard
    nearer = lax.psum_scatter(shard, axes[0], scatter_dimension=dim, tiled=True)
    return scatter_axes(nearer, axes[1:], dim)


def table_entry(table, position):
    return jnp.sum(jnp.where(jnp.arange(table.shape[0]) == position, table, 0))


def split_heads(block_slice):
    return block_slice.reshape(block_slice.shape[0], -1, QUERY_HEADS // KEY_VALUE_HEADS, HEAD_SIZE)


def fresh_state(grouped_heads, token_count):
    array_shape = (grouped_heads, QUERY_HEADS // KEY_VALUE_HEADS, token_count)
    return (
        jnp.full(array_shape, masked_floor, jnp.float32),
        jnp.zeros(array_shape, jnp.float32),
        jnp.zeros(array_shape + (HEAD_SIZE,), jnp.float32),
    )


def absorb(state, query_heads, key_matrix, value_matrix, allowed):
    running_max, running_total, weighted = state
    scores = jnp.einsum(
        "tkgd,nkd->kgtn", query_heads, key_matrix, preferred_element_type=jnp.float32
    ) * (1.0 / math.sqrt(HEAD_SIZE))
    scores = jnp.where(allowed[None, None], scores, -jnp.inf)
    new_max = jnp.maximum(running_max, jnp.max(scores, axis=-1))
    rescale = jnp.exp(running_max - new_max)
    raised = jnp.exp(scores - new_max[..., None])
    new_total = running_total * rescale + jnp.sum(raised, axis=-1)
    update = jnp.einsum(
        "kgtn,nkd->kgtd",
        raised.astype(jnp.bfloat16),
        value_matrix,
        preferred_element_type=jnp.float32,
    )
    return (new_max, new_total, weighted * rescale[..., None] + update)


def absorb_shard(state, query_heads, query_order, shard_rows, shard_index, length, order_all):
    grouped_heads = query_heads.shape[1]
    block_slice = min(key_block, CACHE_DEV)

    def cache_block(number_count, carry):
        begin = number_count * block_slice
        rows = lax.dynamic_slice_in_dim(shard_rows, begin, block_slice, 1)
        key_matrix = rows[0].reshape(block_slice, grouped_heads, HEAD_SIZE)
        value_matrix = rows[1].reshape(block_slice, grouped_heads, HEAD_SIZE)
        allowed = (begin + jnp.arange(block_slice) < length)[None, :]

        def taken(inner):
            return absorb(inner, query_heads, key_matrix, value_matrix, allowed)

        def skipped(inner):
            return inner

        return lax.cond(begin < length, taken, skipped, carry)

    state = lax.fori_loop(0, CACHE_DEV // block_slice, cache_block, state)
    fresh_rows = shard_rows[:, CACHE_DEV:]
    key_order = lax.dynamic_slice_in_dim(
        order_all, shard_index * TOKENS_PER_SHARD, TOKENS_PER_SHARD
    )
    allowed = key_order[None, :] <= query_order[:, None]
    fresh_keys = fresh_rows[0].reshape(TOKENS_PER_SHARD, grouped_heads, HEAD_SIZE)
    fresh_values = fresh_rows[1].reshape(TOKENS_PER_SHARD, grouped_heads, HEAD_SIZE)
    return absorb(state, query_heads, fresh_keys, fresh_values, allowed)


def body(queries, key_value_cache, cache_lengths, token_order, out_weight):
    order_all, lengths_all = (
        lax.all_gather(token_order, "ctx", axis=0, tiled=True),
        lax.all_gather(cache_lengths, "ctx", axis=0, tiled=True),
    )
    device = lax.axis_index("ctx")
    token_count = queries.shape[0]
    grouped_heads = key_value_cache.shape[2] // HEAD_SIZE
    own_order = lax.dynamic_slice_in_dim(order_all, device * TOKENS_PER_SHARD, TOKENS_PER_SHARD)
    query_heads = split_heads(queries)
    piece = lax.all_gather(key_value_cache, "ctx", axis=1, tiled=True)

    def one_shard(number_count, inner):
        rows = lax.dynamic_slice_in_dim(piece, number_count * SHARD_ROWS, SHARD_ROWS, 1)
        return absorb_shard(
            inner,
            query_heads,
            own_order,
            rows,
            number_count,
            table_entry(lengths_all, number_count),
            order_all,
        )

    running_max, total, combined = lax.fori_loop(
        0, piece.shape[1] // SHARD_ROWS, one_shard, fresh_state(grouped_heads, token_count)
    )
    attended = (
        jnp.transpose(combined / total[..., None], (2, 0, 1, 3))
        .reshape(token_count, -1)
        .astype(jnp.bfloat16)
    )
    terms = jnp.dot(
        lax.all_gather(attended, "ctx", axis=0, tiled=True),
        out_weight,
        preferred_element_type=jnp.float32,
    )
    return scatter_axes(terms.astype(jnp.bfloat16), TP, 0).astype(jnp.float32).astype(jnp.bfloat16)


def solution(mesh):
    torus = Mesh(mesh.devices.reshape(mesh.shape["ctx"], 4, 2), ("ctx", "tp_0", "tp_1"))
    return jax.shard_map(
        body,
        mesh=torus,
        in_specs=(P("ctx", TP), P(None, "ctx", TP), P("ctx"), P("ctx"), P(TP, "ctx")),
        out_specs=P(TP, "ctx"),
        check_vma=False,
    )
```

profile of v0, /device:TPU:1, one launch (start us, length us, event | category | flops | bytes accessed | tf_op | source)
XLA Modules:
  0.0 388.7 jit_solution(11620280218035192220)
XLA Ops:
  9.6 21.5 %all-gather = s32[16,1,128]{2,1,0:T(1,128)S(1)} all-gather(s32[1,1,128]{2,1,0:T(1,128)} %bitcast.138), channel_id=1, replica_groups=mesh['ctx'=16,'tp_0'=4,'tp_1'=2] {'ctx'}, dimensions={0}, use_global_device_ids=true | all-gather | bytes 8704 | tf_op jit(solution)/shard_map/all_gather | solution.py:97
  33.1 6.3 %all-reduce = s32[16]{0:T(128)S(1)} all-reduce(s32[16]{0:T(128)S(1)} %dynamic-update-slice), channel_id=1, replica_groups=mesh['ctx'=16,'tp_0'=4,'tp_1'=2] {'ctx'}, use_global_device_ids=true, to_apply=%add | all-reduce | flops 16 | bytes 128
  39.5 12.6 %all-gather.4.cloned.1.call-done = bf16[2,10240,128]{2,1,0:T(8,128)(2,1)} async-done(((bf16[2,640,128]{2,1,0:T(8,128)(2,1)}), bf16[2,10240,128]{2,1,0:T(8,128)(2,1)}) %all-gather.4.cloned.1.call-update) | async-done | bytes 5242896 | tf_op jit(solution)/shard_map/all_gather | solution.py:105
  52.1 179.7 %while.39 = (s32[]{:T(128)}, f32[1,16,128]{2,1,0:T(8,128)S(1)}, f32[1,16,128]{2,1,0:T(8,128)S(1)}, f32[1,16,128,128]{3,2,1,0:T(8,128)}, s32[16]{0:T(128)S(1)}, /...) while((s32[]{:T(128)}, f32[1,16,128]{2,1,0:T(8,128)S(1)}, ...), condition=%wide.region_8.9_spmd.clone, body=%wide.region_0.8_spmd.clone.sunk | while | flops 685802048 | bytes 24371704 | solution.py:119
  54.5 3.9 conditional.3
  59.6 2.3 fusion.49
  65.8 3.9 conditional.3
  70.9 2.3 fusion.49
  77.1 3.9 conditional.3
  88.4 3.9 conditional.3
  93.6 2.3 fusion.49
  99.7 3.9 conditional.3
  104.9 2.3 fusion.49
  111.0 3.9 conditional.3
  122.3 3.9 conditional.3
  127.5 2.3 fusion.49
  133.6 3.9 conditional.3
  138.8 2.3 fusion.49
  145.0 3.9 conditional.3
  156.3 3.9 conditional.3
  161.4 2.3 fusion.49
  167.6 3.9 conditional.3
  172.7 2.3 fusion.49
  178.9 3.9 conditional.3
  190.2 3.9 conditional.3
  201.5 3.9 conditional.3
  212.8 3.9 conditional.3
  224.1 3.9 conditional.3
  234.3 61.2 %all-gather.6.cloned.1.call-done = bf16[2048,2048]{0,1:T(8,128)(2,1)} async-done(((bf16[128,2048]{0,1:T(8,128)(2,1)}), bf16[2048,2048]{0,1:T(8,128)(2,1)}) %all-gather.6.cloned.1.call-update) | async-done | bytes 8388624 | tf_op jit(solution)/shard_map/all_gather | solution.py:128
  295.5 13.9 %convolution_convert_fusion = bf16[2048,1024]{1,0:T(8,128)(2,1)} fusion(bf16[2048,2048]{0,1:T(8,128)(2,1)} %all-gather.6.cloned.1.call-done, bf16[2048,1024]{1,0:T(8,128)(2,1)} %param.13), kind=kOutput, calls=%fused_computation.50 | convolution fusion | flops 8592031744 | bytes 16777216 | tf_op jit(solution)/shard_map/dot_general | solution.py:127
  309.5 46.2 %reduce-scatter.3.cloned.1.call-done = bf16[512,1024]{1,0:T(8,128)(2,1)} async-done(((bf16[2048,1024]{1,0:T(8,128)(2,1)}), bf16[512,1024]{1,0:T(8,128)(2,1)}) %reduce-scatter.3.cloned.1.call-update) | async-done | bytes 1048592 | tf_op jit(solution)/shard_map/reduce_scatter | solution.py:25
  355.8 26.4 %reduce-scatter.5.cloned.1.call-done = bf16[256,1024]{1,0:T(8,128)(2,1)} async-done(((bf16[512,1024]{1,0:T(8,128)(2,1)}), bf16[256,1024]{1,0:T(8,128)(2,1)}) %reduce-scatter.5.cloned.1.call-update) | async-done | bytes 524304 | tf_op jit(solution)/shard_map/reduce_scatter | solution.py:25
  (315 shorter events, 155.7 us)
Async XLA Ops:
  6.5 45.5 %all-gather.4.cloned.1.call-start = ((), (), s32[]{:S(2)}) async-start(), calls=%async_computation.2 | async-start | bytes 5570560 | tf_op jit(solution)/shard_map/all_gather | solution.py:105
  7.3 288.3 %all-gather.6.cloned.1.call-start = ((), (), s32[]{:S(2)}) async-start(), calls=%async_computation.3 | async-start | bytes 8912896 | tf_op jit(solution)/shard_map/all_gather | solution.py:128
  234.3 121.5 %reduce-scatter.3.cloned.1.call-start = ((), (), s32[]{:S(2)}) async-start(), calls=%async_computation.4 | async-start | bytes 5242880 | tf_op jit(solution)/shard_map/reduce_scatter | solution.py:25
  309.5 72.7 %reduce-scatter.5.cloned.1.call-start = ((), (), s32[]{:S(2)}) async-start(), calls=%async_computation.5 | async-start | bytes 1572864 | tf_op jit(solution)/shard_map/reduce_scatter | solution.py:25
Sparse Core Ops, SparseCore 0:
  9.0 43.0 all-gather.3
  234.4 61.0 all-gather.5
  309.6 46.1 reduce-scatter.2
  358.0 24.1 reduce-scatter.4
where the time goes:
time: 393 us; the launch traced here: 389 us
  waiting for transfers between devices  147 us (37%)
  matrix products  104 us (26%)
  other arithmetic  60.6 us (15%)
  blocking collectives  27.9 us (7%)
  local copies, waits for them, and re-layouts  22.5 us (6%)
  between operations  13.8 us (4%)
  loops' own time  12.6 us (3%)
    reduce_scatter x2, waiting for transfers between devices, scatter_axes(): nearer = lax.psum_scatter(shard, axes[0], scatter_dimension=dim, tiled=True)  72.6 us
    all_gather x1, waiting for transfers between devices, body(): lax.all_gather(attended, 'ctx', axis=0, tiled=True)  61.2 us
    dot_general x32, matrix products, absorb(): jnp.einsum('kgtn,nkd->kgtd', raised.astype(jnp.bfloat16), value_matrix, p...  61.2 us
    dot_general x32, matrix products, absorb(): jnp.einsum('tkgd,nkd->kgtn', query_heads, key_matrix, preferred_element_t...  28.9 us
    all_gather x1, blocking collectives, body(): lax.all_gather(token_order, 'ctx', axis=0, tiled=True)  21.5 us
    while x32, other arithmetic  19.8 us
    reduce_sum x32, other arithmetic, absorb(): new_total = running_total * rescale + jnp.sum(raised, axis=-1)  17.2 us
    dynamic_slice x16, local copies, waits for them, and re-layouts, one_shard(): lax.dynamic_slice_in_dim(piece, number_count * SHARD_ROWS, SHARD_ROWS, 1)  16.1 us
  transfers between devices with their start and end apart: 4, of which 4 were waited for; matrix products, arithmetic and copies ran while one was open for 1% of the time, Pallas kernels for 0%

commit v1 on v0

v1 whole, which is shorter than its diff:
```python
import math
import jax
import jax.numpy as jnp
from jax import lax
from jax.sharding import Mesh
from jax.sharding import PartitionSpec as P
from jax.experimental import pallas as pl
from jax.experimental.pallas import tpu as pltpu

HEAD_SIZE = 128
UNIT = 128
BLOCK = 512
TILE = 256
CACHE_DEV = 512
SHARD_ROWS = 640
SHARDS = 16
V_ROWS = 144
FLOOR = -1e30
TO_EXP2 = math.log2(math.e) / math.sqrt(HEAD_SIZE)


def attend_kernel(lens, order, own, q, kv, out, keys, values, queries, peak, acc):
    heads = q.shape[1] // HEAD_SIZE
    unit_rows = lax.broadcasted_iota(jnp.int32, (UNIT, HEAD_SIZE), 0)
    v_rows = lax.broadcasted_iota(jnp.int32, (V_ROWS - HEAD_SIZE, UNIT), 0)
    v_lanes = lax.broadcasted_iota(jnp.int32, (V_ROWS - HEAD_SIZE, UNIT), 1)
    lanes = lax.broadcasted_iota(jnp.int32, (HEAD_SIZE, UNIT), 1)

    for h in range(heads):
        queries[:, h * UNIT:(h + 1) * UNIT] = q[:, h * HEAD_SIZE:(h + 1) * HEAD_SIZE].T

    def put(at, key_unit, value_unit, left):
        keys[pl.ds(at, UNIT), :] = key_unit
        values[:HEAD_SIZE, pl.ds(at, UNIT)] = jnp.where(lanes < left, value_unit, 0).astype(jnp.bfloat16)
        values[HEAD_SIZE:, pl.ds(at, UNIT)] = jnp.where((v_rows == 0) & (v_lanes < left), 1.0, 0.0).astype(jnp.bfloat16)

    def fresh_unit(s, carry):
        at = pl.multiple_of(s * SHARD_ROWS + CACHE_DEV, UNIT)
        put(pl.multiple_of(s * UNIT, UNIT), kv[0, pl.ds(at, UNIT), :], kv[1, pl.ds(at, UNIT), :].T, UNIT)
        return carry

    lax.fori_loop(0, SHARDS, fresh_unit, 0)

    def shard_units(s, used):
        base = pl.multiple_of(s * SHARD_ROWS, UNIT)
        length = lens[s]
        first = jnp.broadcast_to(kv[0, pl.ds(base, 16), :][:1], (UNIT, HEAD_SIZE))

        def unit(b, used):
            at = pl.multiple_of(base + b * UNIT, UNIT)
            left = length - b * UNIT
            key_unit = jnp.where(unit_rows < left, kv[0, pl.ds(at, UNIT), :], first)
            put(pl.multiple_of(used, UNIT), key_unit, kv[1, pl.ds(at, UNIT), :].T, left)
            return used + UNIT

        return lax.fori_loop(0, (length + UNIT - 1) // UNIT, unit, used)

    used = lax.fori_loop(0, SHARDS, shard_units, SHARDS * UNIT)
    blocks = (used + BLOCK - 1) // BLOCK
    spare = jnp.broadcast_to(kv[0, 0:16, :][:1], (UNIT, HEAD_SIZE))
    nothing = jnp.zeros((HEAD_SIZE, UNIT), jnp.bfloat16)

    def pad(i, carry):
        put(pl.multiple_of(used + i * UNIT, UNIT), spare, nothing, 0)
        return carry

    lax.fori_loop(0, (blocks * BLOCK - used) // UNIT, pad, 0)

    peak[...] = jnp.full(peak.shape, FLOOR, jnp.float32)
    acc[...] = jnp.zeros(acc.shape, jnp.float32)

    def absorb(at, allowed):
        key_block = keys[pl.ds(at, BLOCK), :]
        value_block = values[:, pl.ds(at, BLOCK)]
        for t in range(heads * UNIT // TILE):
            cols = slice(t * TILE, (t + 1) * TILE)
            scores = jnp.dot(key_block, queries[:, cols], preferred_element_type=jnp.float32)
            if allowed is not None:
                scores = jnp.where(allowed, scores, FLOOR)
            old = peak[:, cols]
            new = jnp.maximum(old, jnp.max(scores, axis=0, keepdims=True))
            weights = jnp.exp2((scores - new) * TO_EXP2).astype(jnp.bfloat16)
            acc[:, cols] = acc[:, cols] * jnp.exp2((old - new) * TO_EXP2) + jnp.dot(
                value_block, weights, preferred_element_type=jnp.float32
            )
            peak[:, cols] = new

    def cache_block(i, carry):
        absorb(pl.multiple_of(i * BLOCK, BLOCK), None)
        return carry

    lax.fori_loop(SHARDS * UNIT // BLOCK, blocks, cache_block, 0)

    own_row = own[...]

    def fresh_block(i, carry):
        rows = []
        for j in range(BLOCK // UNIT):
            row = order[pl.ds(i * (BLOCK // UNIT) + j, 1), :]
            rows.append(jnp.broadcast_to(row, (UNIT, UNIT)).T)
        column = jnp.concatenate(rows, axis=0)
        allowed = column <= own_row
        allowed = jnp.concatenate([allowed] * (TILE // UNIT), axis=1)
        absorb(pl.multiple_of(i * BLOCK, BLOCK), allowed)
        return carry

    lax.fori_loop(0, SHARDS * UNIT // BLOCK, fresh_block, 0)

    for h in range(heads):
        cols = slice(h * UNIT, (h + 1) * UNIT)
        done = acc[:HEAD_SIZE, cols] / acc[HEAD_SIZE:HEAD_SIZE + 1, cols]
        out[:, h * HEAD_SIZE:(h + 1) * HEAD_SIZE] = done.T.astype(jnp.bfloat16)


def attend(lens, order, own, q, kv):
    rows = kv.shape[1]
    width = q.shape[1]
    vmem = pl.BlockSpec(memory_space=pltpu.VMEM)
    return pl.pallas_call(
        attend_kernel,
        out_shape=jax.ShapeDtypeStruct(q.shape, jnp.bfloat16),
        in_specs=[pl.BlockSpec(memory_space=pltpu.SMEM), vmem, vmem, vmem, vmem],
        out_specs=vmem,
        scratch_shapes=[
            pltpu.VMEM((rows, HEAD_SIZE), jnp.bfloat16),
            pltpu.VMEM((V_ROWS, rows), jnp.bfloat16),
            pltpu.VMEM((HEAD_SIZE, width), jnp.bfloat16),
            pltpu.VMEM((1, width), jnp.float32),
            pltpu.VMEM((V_ROWS, width), jnp.float32),
        ],
        compiler_params=pltpu.CompilerParams(vmem_limit_bytes=48 * 2**20),
    )(lens, order, own, q, kv)


TP = ("tp_0", "tp_1")
TOKENS_PER_SHARD = 128


def body(queries, key_value_cache, cache_lengths, token_order, out_weight):
    gathered = lax.all_gather(key_value_cache, "ctx", axis=1, tiled=True)
    facts = jnp.concatenate([token_order, jnp.broadcast_to(cache_lengths, (128,))])[None]
    facts = lax.all_gather(facts, "ctx", axis=0, tiled=True)
    attended = attend(facts[:, 128], facts[:, :128].astype(jnp.float32), token_order[None].astype(jnp.float32), queries, gathered)
    terms = jnp.dot(
        lax.all_gather(attended, "ctx", axis=0, tiled=True),
        out_weight,
        preferred_element_type=jnp.float32,
    ).astype(jnp.bfloat16)
    terms = lax.psum_scatter(terms, "tp_0", scatter_dimension=0, tiled=True)
    return lax.psum_scatter(terms, "tp_1", scatter_dimension=0, tiled=True)


def solution(mesh):
    torus = Mesh(mesh.devices.reshape(mesh.shape["ctx"], 4, 2), ("ctx", "tp_0", "tp_1"))
    return jax.shard_map(
        body,
        mesh=torus,
        in_specs=(P("ctx", TP), P(None, "ctx", TP), P("ctx"), P("ctx"), P(TP, "ctx")),
        out_specs=P(TP, "ctx"),
        check_vma=False,
    )
```

time: 393 us -> 245 us (0.62); the launches traced: 389 us -> 247 us
  matrix products: 104 us -> 13.8 us
  other arithmetic: 60.6 us -> 0.66 us
  Pallas kernels: 0 us -> 47.4 us
  local copies, waits for them, and re-layouts: 22.5 us -> 1.82 us
  loops' own time: 12.6 us -> 0 us
  blocking collectives: 27.9 us -> 21.4 us
    dot_general x64 -> x0, matrix products: 90 us -> none  [the longest x32 61.2 us: absorb(): jnp.einsum('kgtn,nkd->kgtd', raised.astype(jnp.bfloat16), value_matrix, p...]
    pallas_call x0 -> x1, Pallas kernels: none -> 47.4 us  [attend(): pl.pallas_call(attend_kernel, out_shape=jax.ShapeDtypeStruct(q.shape, jnp...]
    reduce_sum x48 -> x0, other arithmetic: 27.7 us -> none  [the longest x32 17.2 us: absorb(): new_total = running_total * rescale + jnp.sum(raised, axis=-1)]
    while x32 -> x0, other arithmetic: 19.8 us -> none
    dynamic_slice x33 -> x0, local copies, waits for them, and re-layouts: 17.4 us -> none  [the longest x16 16.1 us: one_shard(): lax.dynamic_slice_in_dim(piece, number_count * SHARD_ROWS, SHARD_ROWS, 1)]
    another operation x17 -> x0, loops' own time: 12.6 us -> none  [the longest x1 11.7 us: body(): lax.fori_loop(0, piece.shape[1] // SHARD_ROWS, one_shard, fresh_state(gro...]
    lt x16 -> x0, other arithmetic: 10.2 us -> none  [cache_block(): allowed = (begin + jnp.arange(block_slice) < length)[None, :]]
    all_gather x1, waiting for transfers between devices: 61.2 us -> 52.4 us  [body(): lax.all_gather(attended, 'ctx', axis=0, tiled=True)]
where the time goes in v1:
time: 245 us; the launch traced here: 247 us
  waiting for transfers between devices  148 us (60%)
  Pallas kernels  47.4 us (19%)
  blocking collectives  21.4 us (9%)
  matrix products  13.8 us (6%)
  between operations  13.8 us (6%)
    all_gather x1, waiting for transfers between devices, body(): lax.all_gather(attended, 'ctx', axis=0, tiled=True)  52.4 us
    pallas_call x1, Pallas kernels, attend(): pl.pallas_call(attend_kernel, out_shape=jax.ShapeDtypeStruct(q.shape, jnp...  47.4 us
    reduce_scatter x1, waiting for transfers between devices, body(): terms = lax.psum_scatter(terms, 'tp_0', scatter_dimension=0, tiled=True)  47.3 us
    reduce_scatter x1, waiting for transfers between devices, body(): return lax.psum_scatter(terms, 'tp_1', scatter_dimension=0, tiled=True)  26.4 us
    all_gather x1, blocking collectives, body(): facts = lax.all_gather(facts, 'ctx', axis=0, tiled=True)  21.4 us
    all_gather x1, waiting for transfers between devices, body(): gathered = lax.all_gather(key_value_cache, 'ctx', axis=1, tiled=True)  21 us
    dot_general x1, matrix products, body(): jnp.dot(lax.all_gather(attended, 'ctx', axis=0, tiled=True), out_weight,...  13.8 us
  transfers between devices with their start and end apart: 4, of which 4 were waited for; matrix products, arithmetic and copies ran while one was open for 1% of the time, Pallas kernels for 0%

profile of v1, /device:TPU:1, one launch (start us, length us, event | category | flops | bytes accessed | tf_op | source)
XLA Modules:
  0.0 246.8 jit_solution(4916933234235394428)
XLA Ops:
  6.5 0.0 all-gather.5.cloned.1.call-start
  6.5 0.7 all-gather.5.cloned.1.call-update
  7.3 0.0 all-gather.7.cloned.1.call-start
  7.9 0.7 concatenate.3
  8.6 21.4 %all-gather.1 = s32[16,1,256]{2,1,0:T(1,128)S(1)} all-gather(s32[1,1,256]{2,1,0:T(1,128)S(1)} %bitcast.12), channel_id=2, replica_groups=mesh['ctx'=16,'tp_0'=4,'tp_1'=2] {'ctx'}, dimensions={0}, use_global_device_ids=true | all-gather | bytes 17408 | tf_op jit(solution)/shard_map/all_gather | solution.py:142
  30.0 0.1 slice_reduce_fusion.lens
  30.1 0.7 convert_bitcast_fusion.own
  30.8 21.0 %all-gather.5.cloned.1.call-done.kv = bf16[2,10240,128]{2,1,0:T(8,128)(2,1)} async-done(((bf16[2,640,128]{2,1,0:T(8,128)(2,1)}), bf16[2,10240,128]{2,1,0:T(8,128)(2,1)}) %all-gather.5.cloned.1.call-update) | async-done | bytes 5242896 | tf_op jit(solution)/shard_map/all_gather | solution.py:140
  51.8 0.0 copy-start
  51.8 1.0 copy-done
  52.8 47.4 %shard_map.55 = bf16[128,2048]{1,0:T(8,128)(2,1)} custom-call(s32[16]{0:T(128)S(1)} %slice_reduce_fusion.lens, f32[16,128]{1,0:T(8,128)S(1)} %slice_convert_fusion.order, f32[1,128]{1,0:T(1,128)S(1)} %convert_bitcast_fusion.own, bf16[128,2048]{1,0:T(8,128)(2,1)S(1)} %copy-done, bf16[2,10240,128]{2,1,0:T(8,128)(2,1)} %all-gather.5.cloned.1.call-done.kv), custom_call_target="tpu_custom_call" | custom-call | tf_op jit(solution)/shard_map/pallas_call | solution.py:119
  100.3 0.0 all-gather.7.cloned.1.call-update
  100.3 0.0 reduce-scatter.3.cloned.1.call-start
  100.3 52.4 %all-gather.7.cloned.1.call-done = bf16[2048,2048]{1,0:T(8,128)(2,1)} async-done(((bf16[128,2048]{1,0:T(8,128)(2,1)}), bf16[2048,2048]{1,0:T(8,128)(2,1)}) %all-gather.7.cloned.1.call-update) | async-done | bytes 8388624 | tf_op jit(solution)/shard_map/all_gather | solution.py:145
  152.7 13.8 %convolution_convert_fusion = bf16[2048,1024]{1,0:T(8,128)(2,1)} fusion(bf16[2048,2048]{1,0:T(8,128)(2,1)} %all-gather.7.cloned.1.call-done, bf16[2048,1024]{1,0:T(8,128)(2,1)} %param.9), kind=kOutput, calls=%fused_computation | convolution fusion | flops 8592031744 | bytes 16777216 | tf_op jit(solution)/shard_map/dot_general | solution.py:144
  166.5 0.0 reduce-scatter.3.cloned.1.call-update
  166.5 0.0 reduce-scatter.5.cloned.1.call-start
  166.6 47.3 %reduce-scatter.3.cloned.1.call-done = bf16[512,1024]{1,0:T(8,128)(2,1)} async-done(((bf16[2048,1024]{1,0:T(8,128)(2,1)}), bf16[512,1024]{1,0:T(8,128)(2,1)}) %reduce-scatter.3.cloned.1.call-update) | async-done | bytes 1048592 | tf_op jit(solution)/shard_map/reduce_scatter | solution.py:149
  213.9 0.0 reduce-scatter.5.cloned.1.call-update
  213.9 26.4 %reduce-scatter.5.cloned.1.call-done = bf16[256,1024]{1,0:T(8,128)(2,1)} async-done(((bf16[512,1024]{1,0:T(8,128)(2,1)}), bf16[256,1024]{1,0:T(8,128)(2,1)}) %reduce-scatter.5.cloned.1.call-update) | async-done | bytes 524304 | tf_op jit(solution)/shard_map/reduce_scatter | solution.py:150
  (2 shorter events, 0.0 us)
Async XLA Ops:
  6.5 45.2 %all-gather.5.cloned.1.call-start = ((), (), s32[]{:S(2)}) async-start(), calls=%async_computation.2 | async-start | bytes 5570560 | tf_op jit(solution)/shard_map/all_gather | solution.py:140
  7.3 145.5 %all-gather.7.cloned.1.call-start = ((), (), s32[]{:S(2)}) async-start(), calls=%async_computation.3 | async-start | bytes 8912896 | tf_op jit(solution)/shard_map/all_gather | solution.py:145
  51.8 1.0 copy-start
  100.3 113.6 %reduce-scatter.3.cloned.1.call-start = ((), (), s32[]{:S(2)}) async-start(), calls=%async_computation.4 | async-start | bytes 5242880 | tf_op jit(solution)/shard_map/reduce_scatter | solution.py:149
  166.5 73.8 %reduce-scatter.5.cloned.1.call-start = ((), (), s32[]{:S(2)}) async-start(), calls=%async_computation.5 | async-start | bytes 1572864 | tf_op jit(solution)/shard_map/reduce_scatter | solution.py:150
Sparse Core Ops, SparseCore 0:
  9.0 42.7 all-gather.4
  100.4 52.2 all-gather.6
  166.6 47.1 reduce-scatter.2
  216.1 24.1 reduce-scatter.4
